TPU v7x, 32 devices: a whole 2x2x4 slice. The times are simulated.
32 devices in a mesh: mem: 8 (over z, x), chan: 4 (over y, core).
Axes of the slice: x: 2, y: 2, z: 4, core: 2. Of those that a mesh axis runs over, the one named last changes fastest.
Arguments:
- state_anom: bfloat16 [8, 64, 137], P(None, 'mem'), may hold values from -6 to 6
- radiance_anom: bfloat16 [8, 64, 8704], P(None, 'mem', 'chan'), may hold values from -6 to 6
- inv_noise: float32 [8704], P('chan'), may hold values from 0.02 to 0.2
- innovation: float32 [8, 8704], P(None, 'chan'), may hold values from -6 to 6
- valid_count: int32 [8], replicated, may hold values from 4352 to 8461
Outputs:
- information: float32 [8, 137, 137], P('mem')
- gradient: float32 [8, 137], P('mem')
- increment: float32 [8, 137], P('mem')
All inputs are finite; a program needn't handle non-finite values.
Results may differ from a plain program's by a relative error of at most 0.0003.
Values may be sent and summed in bfloat16 or wider, within the bound.
A program may use at most 64 MiB of HBM per device.

v0:
```python
import jax
import jax.numpy as jnp
from jax import lax
from jax.sharding import PartitionSpec as P


def slab_terms(cross, weight, innov_rows):
    weighted = cross * weight[:, :, None]
    info_part = jnp.einsum("pcs,pct->pst", weighted, cross, precision=lax.Precision.HIGHEST)
    grad_part = jnp.einsum("pcs,pc->ps", weighted, innov_rows, precision=lax.Precision.HIGHEST)
    return (info_part, grad_part)


def shards(state_anom, radiance_anom, inv_noise, innovation, valid_count):
    profiles = state_anom.shape[0]
    states = state_anom.shape[2]
    slab_width = radiance_anom.shape[2]
    members_all = state_anom.shape[1] * lax.axis_size("mem")
    prof_local = profiles // lax.axis_size("mem")
    slab_start = lax.axis_index("chan") * slab_width
    own_rad, own_states = (
        lax.all_to_all(radiance_anom, "mem", split_axis=0, concat_axis=1, tiled=True),
        lax.all_to_all(state_anom, "mem", split_axis=0, concat_axis=1, tiled=True),
    )
    cross = jnp.einsum("pmc,pms->pcs", own_rad, own_states, preferred_element_type=jnp.float32)
    cross = cross / jnp.float32(members_all - 1)
    first_prof = lax.axis_index("mem") * prof_local
    own_count = lax.dynamic_slice_in_dim(valid_count, first_prof, prof_local, 0)
    slots = slab_start + jnp.arange(slab_width, dtype=jnp.int32)
    valid = (slots[None, :] < own_count[:, None]).astype(jnp.float32)
    weight = inv_noise[None, :] * valid
    innov_rows = lax.dynamic_slice_in_dim(innovation, first_prof, prof_local, 0)
    info_share, grad_share = slab_terms(cross, weight, innov_rows)
    information, gradient = lax.psum((info_share, grad_share), "chan")
    system = information + jnp.eye(states, dtype=jnp.float32)[None]
    factor = jnp.linalg.cholesky(system)
    increment = jax.scipy.linalg.cho_solve((factor, True), gradient[:, :, None])[:, :, 0]
    return (information, gradient, increment)


def solution(mesh):
    in_specs = (P(None, "mem", None), P(None, "mem", "chan"), P("chan"), P(None, "chan"), P())
    out_specs = (P("mem", None, None), P("mem", None), P("mem", None))
    return jax.shard_map(shards, mesh=mesh, in_specs=in_specs, out_specs=out_specs, check_vma=False)
```

profile of v0, /device:TPU:0, one launch (start us, length us, event | category | flops | bytes accessed | tf_op | source)
XLA Modules:
  0.0 121.7 jit_solution(8152377795422508364)
XLA Ops:
  7.2 0.0 copy-start
  7.2 14.1 %all_to_all.8 = bf16[8,8,137]{2,1,0:T(8,128)(2,1)S(1)} all-to-all(bf16[8,8,137]{2,1,0:T(8,128)(2,1)} %param.5), channel_id=1, replica_groups=mesh['mem'=8,'chan'=4] {'mem'}, dimensions={0} | all-to-all | bytes 35072 | tf_op jit(solution)/shard_map/all_to_all | solution.py:23
  21.3 3.4 %all-to-all-start = ((bf16[8,8,2176]{2,1,0:T(8,128)(2,1)}), bf16[8,8,2176]{2,1,0:T(8,128)(2,1)S(1)}, u32[]{:S(2)}, u32[]{:S(2)}) async-start(bf16[8,8,2176]{2,1,0:T(8,128)(2,1)} %param.6), calls=%async_computation | async-start | bytes 557056 | tf_op jit(solution)/shard_map/all_to_all | solution.py:22
  24.7 0.0 all-reduce.5.cloned.1.call-start
  24.8 1.2 %dynamic_slice.6 = s32[1]{0:T(128)} dynamic-slice(s32[8]{0:T(128)} %param.9, s32[]{:T(128)S(6)} %select_n.8), dynamic_slice_sizes={1} | dynamic-slice | bytes 12 | tf_op jit(solution)/shard_map/dynamic_slice | solution.py:28
  26.1 1.4 %select_multiply_fusion = f32[2176]{0:T(1024)S(1)} fusion(f32[2176]{0:T(1024)} %param.7, s32[]{:T(128)} %bitcast.1, s32[]{:T(128)S(6)} %mul.19), kind=kLoop, calls=%fused_computation.43 | loop fusion | flops 8704 | bytes 17416 | tf_op jit(solution)/shard_map/mul | solution.py:8
  27.4 5.6 %all-to-all-done = bf16[8,8,2176]{2,1,0:T(8,128)(2,1)S(1)} async-done(((bf16[8,8,2176]{2,1,0:T(8,128)(2,1)}), bf16[8,8,2176]{2,1,0:T(8,128)(2,1)S(1)}, u32[]{:S(2)}, u32[]{:S(2)}) %all-to-all-start) | async-done | bytes 278560 | tf_op jit(solution)/shard_map/all_to_all | solution.py:22
  33.0 0.4 convolution_bitcast_fusion
  33.4 1.9 %fusion.5 = f32[1,137,137]{1,2,0:T(8,128)} fusion(f32[2176,137]{0,1:T(8,128)S(1)} %convolution_bitcast_fusion, f32[2176]{0:T(1024)S(1)} %select_multiply_fusion), kind=kOutput, calls=%fused_computation.6 | convolution fusion | flops 490692352 | bytes 1276228 | tf_op jit(solution)/shard_map/pcs,pct->pst/dot_general | solution.py:9
  35.3 0.0 all-reduce.5.cloned.1.call-update
  35.3 0.0 copy-done
  35.3 1.1 fusion.2
  36.5 5.8 %psum.15 = f32[1,137]{1,0:T(1,128)S(1)} all-reduce(f32[1,137]{1,0:T(1,128)S(1)} %fusion.2), channel_id=1, replica_groups=mesh['mem'=8,'chan'=4] {'chan'}, use_global_device_ids=true, to_apply=%region_1.0 | all-reduce | flops 137 | bytes 1096 | tf_op jit(solution)/shard_map/psum | solution.py:34
  42.3 0.0 copy-start.2
  42.3 23.1 %all-reduce.5.cloned.1.call-done = f32[1,137,137]{1,2,0:T(8,128)} async-done(((f32[1,137,137]{1,2,0:T(8,128)}), f32[1,137,137]{1,2,0:T(8,128)}) %all-reduce.5.cloned.1.call-update) | async-done | bytes 75092 | tf_op jit(solution)/shard_map/psum | solution.py:34
  65.4 0.9 convert_add_fusion
  66.3 0.0 copy-start.1
  66.3 0.1 copy.9
  66.4 0.9 fusion.18
  67.4 11.7 %custom-call.20 = f32[1,128,128]{2,1,0:T(8,128)S(1)} custom-call(f32[1,128,128]{2,1,0:T(8,128)S(1)} %cholesky.123), custom_call_target="Cholesky" | custom-call | tf_op jit(solution)/shard_map/jit(cholesky)/cholesky | solution.py:36
  79.2 9.8 %custom-call.21 = f32[1,1,128,128]{2,3,1,0:T(8,128)S(1)} custom-call(f32[1,1,128,128]{3,2,1,0:T(8,128)S(1)} %get-tuple-element.27), custom_call_target="InvertDiagBlocksLowerTriangular" | custom-call | tf_op jit(solution)/shard_map/jit(cholesky)/cholesky | solution.py:36
  89.0 0.2 bitcast_dynamic-update-slice_fusion
  89.1 0.1 fusion.10
  89.3 0.8 custom-call.22
  90.1 0.7 compare_reduce_fusion.1
  90.8 0.6 compare_reduce_fusion
  92.7 0.1 fusion.19
  92.9 19.7 %custom-call.23 = f32[2,128,128]{1,2,0:T(8,128)S(1)} custom-call(f32[2,128,128]{2,1,0:T(8,128)S(1)} %pad_maximum_fusion), custom_call_target="InvertDiagBlocksLowerTriangular" | custom-call | tf_op jit(solution)/shard_map/jit(_cho_solve)/triangular_solve | solution.py:37
  112.5 0.2 fusion.22
  112.7 0.0 copy-done.2
  112.7 0.1 fusion.14
  112.8 0.1 convolution_bitcast_fusion.5
  113.0 0.1 convolution_bitcast_fusion.4
  113.1 0.1 fusion.12
  113.3 0.2 convolution_bitcast_fusion.2
  113.5 0.6 maximum_bitcast_fusion
  114.1 0.0 copy-done.1
  114.1 0.8 copy.11
  (9 shorter events, 0.1 us)
Async XLA Ops:
  7.2 28.2 %copy-start = (f32[8,2176]{1,0:T(8,128)S(1)}, f32[8,2176]{1,0:T(8,128)}, u32[]{:S(2)}) copy-start(f32[8,2176]{1,0:T(8,128)} %param.8) | copy-start | bytes 208900
  21.3 11.7 %all-to-all-start = ((bf16[8,8,2176]{2,1,0:T(8,128)(2,1)}), bf16[8,8,2176]{2,1,0:T(8,128)(2,1)S(1)}, u32[]{:S(2)}, u32[]{:S(2)}) async-start(bf16[8,8,2176]{2,1,0:T(8,128)(2,1)} %param.6), calls=%async_computation | async-start | bytes 557056 | tf_op jit(solution)/shard_map/all_to_all | solution.py:22
  24.7 40.7 %all-reduce.5.cloned.1.call-start = ((), (), s32[]{:S(2)}) async-start(), calls=%async_computation.2 | async-start | bytes 294912 | tf_op jit(solution)/shard_map/psum | solution.py:34
  42.3 70.4 %copy-start.2 = (f32[1,137]{1,0:T(1,128)}, f32[1,137]{1,0:T(1,128)S(1)}, u32[]{:S(2)}) copy-start(f32[1,137]{1,0:T(1,128)S(1)} %psum.15) | copy-start | bytes 1648
  66.3 47.8 %copy-start.1 = (f32[1,137,137]{1,2,0:T(8,128)S(1)}, f32[1,137,137]{1,2,0:T(8,128)}, u32[]{:S(2)}) copy-start(f32[1,137,137]{1,2,0:T(8,128)} %all-reduce.5.cloned.1.call-done) | copy-start | bytes 225232
Sparse Core Ops, SparseCore 0:
  35.5 29.8 all-reduce.4
where the time goes:
time: 122 us
  other arithmetic  47.4 us (39%)
  waiting for transfers between devices  28.7 us (24%)
  blocking collectives  19.9 us (16%)
  between operations  15.5 us (13%)
  matrix products  4.67 us (4%)
  starting transfers between devices  3.46 us (3%)
  local copies, waits for them, and re-layouts  2.15 us (2%)
    another operation x7, other arithmetic, shards(): factor = jnp.linalg.cholesky(system)  23.7 us
    psum x1, waiting for transfers between devices, shards(): information, gradient = lax.psum((info_share, grad_share), 'chan')  23.1 us
    another operation x6, other arithmetic, shards(): jax.scipy.linalg.cho_solve((factor, True), gradient[:, :, None])[:, :, 0]  19.8 us
    all_to_all x1, blocking collectives, shards(): lax.all_to_all(state_anom, 'mem', split_axis=0, concat_axis=1, tiled=True)  14.1 us
    psum x1, blocking collectives, shards(): information, gradient = lax.psum((info_share, grad_share), 'chan')  5.84 us
    all_to_all x1, waiting for transfers between devices, shards(): lax.all_to_all(radiance_anom, 'mem', split_axis=0, concat_axis=1, tiled=T...  5.57 us
    all_to_all x1, starting transfers between devices, shards(): lax.all_to_all(radiance_anom, 'mem', split_axis=0, concat_axis=1, tiled=T...  3.42 us
  transfers between devices with their start and end apart: 2, of which 2 were waited for; matrix products, arithmetic and copies ran while one was open for 3% of the time, Pallas kernels for 0%

commit v1 on v0

v1 whole, which is shorter than its diff:
```python
import functools
import jax
import jax.numpy as jnp
from jax import lax
from jax.experimental import pallas as pl
from jax.experimental.pallas import tpu as pltpu
from jax.sharding import PartitionSpec as P

F32, BF16 = jnp.float32, jnp.bfloat16
LANES, SUB = 128, 8
VMEM_LIMIT = 60 * 1024 * 1024


def up(x, to):
    return -(-x // to) * to


def split3(x):
    a = x.astype(BF16)
    rest = x - a.astype(F32)
    b = rest.astype(BF16)
    c = (rest - b.astype(F32)).astype(BF16)
    return a, b, c


def gram_kernel(n_mem, n_chan, count_ref, state_ref, rad_ref, noise_ref, innov_ref,
                gram_ref, states_ref, held, held_states, innov, parts,
                local_sem, send_sem, recv_sem, ssend_sem, srecv_sem, psend_sem, precv_sem):
    me, slab = lax.axis_index("mem"), lax.axis_index("chan")
    members = rad_ref.shape[1]
    width = rad_ref.shape[2]
    total = n_mem * members
    columns = parts.shape[2]

    barrier = pltpu.get_barrier_semaphore()
    for k in range(1, n_mem):
        pl.semaphore_signal(barrier, inc=1, device_id={"mem": lax.rem(me + k, n_mem)})
    for k in range(1, n_chan):
        pl.semaphore_signal(barrier, inc=1, device_id={"chan": lax.rem(slab + k, n_chan)})
    own = [
        pltpu.make_async_copy(rad_ref.at[me], held.at[0], local_sem.at[0]),
        pltpu.make_async_copy(state_ref.at[me], held_states.at[0], local_sem.at[1]),
        pltpu.make_async_copy(innov_ref, innov, local_sem.at[2]),
    ]
    for copy in own:
        copy.start()
    pl.semaphore_wait(barrier, n_mem - 1 + n_chan - 1)

    sends = []
    for k in range(1, n_mem):
        peer = lax.rem(me + k, n_mem)
        sends.append(pltpu.make_async_remote_copy(
            src_ref=rad_ref.at[peer], dst_ref=held.at[k],
            send_sem=send_sem.at[k], recv_sem=recv_sem.at[k], device_id={"mem": peer}))
        sends[-1].start()
    for k in range(1, n_mem):
        peer = lax.rem(me + k, n_mem)
        sends.append(pltpu.make_async_remote_copy(
            src_ref=state_ref.at[peer], dst_ref=held_states.at[k],
            send_sem=ssend_sem.at[k], recv_sem=srecv_sem.at[k], device_id={"mem": peer}))
        sends[-1].start()

    for copy in own:
        copy.wait()
    slots = slab * width + lax.broadcasted_iota(jnp.int32, (1, width), 1)
    weight = jnp.where(slots < count_ref[me], noise_ref[...], 0.0)
    pull = weight * innov[pl.ds(me, 1), :]
    pull = [part.astype(F32) for part in split3(pull)]
    for copy in sends:
        copy.wait_recv()

    extra = columns - total
    row = lax.broadcasted_iota(jnp.int32, (extra, 1), 0)
    acc = jnp.zeros((total, columns), F32)
    step = 2 * LANES
    for lo in range(0, width, step):
        hi = min(lo + step, width)
        block = held[:, :, lo:hi].astype(F32).reshape(total, hi - lo)
        scaled = block * weight[:, lo:hi]
        first = scaled.astype(BF16)
        second = (scaled - first.astype(F32)).astype(BF16)
        p0, p1, p2 = (part[:, lo:hi] for part in pull)
        tail0 = jnp.where(row == 0, p0, jnp.where(row == 1, p2, 0.0)).astype(BF16)
        tail1 = jnp.where(row == 0, p1, 0.0).astype(BF16)
        block = block.astype(BF16)
        dims = (((1,), (1,)), ((), ()))
        acc += (
            lax.dot_general(block, jnp.concatenate([first, tail0], 0), dims, preferred_element_type=F32)
            + lax.dot_general(block, jnp.concatenate([second, tail1], 0), dims, preferred_element_type=F32)
        )
    parts[slab] = acc
    states_ref[...] = held_states[...]

    shares = []
    for k in range(1, n_chan):
        peer = lax.rem(slab + k, n_chan)
        shares.append(pltpu.make_async_remote_copy(
            src_ref=parts.at[slab], dst_ref=parts.at[slab],
            send_sem=psend_sem.at[k], recv_sem=precv_sem.at[k], device_id={"chan": peer}))
        shares[-1].start()
    for copy in sends:
        copy.wait_send()
    for copy in shares:
        copy.wait()
    whole = parts[0]
    for k in range(1, n_chan):
        whole = whole + parts[k]
    gram_ref[...] = whole


def eliminate(system, order):
    rows, lanes = system.shape
    rid = lax.broadcasted_iota(jnp.int32, (SUB, LANES), 0)

    def wide(piece, tiles):
        return piece if tiles == 1 else jnp.concatenate([piece] * tiles, 1)

    for p in range(0, order, SUB):
        steps = min(SUB, order - p)
        base = p // LANES * LANES
        live = system[:, base:]
        tiles = (lanes - base) // LANES
        cols = []
        for j in range(steps):
            at = p - base + j
            full = jnp.broadcast_to(live[:, at:at + 1], (rows, LANES))
            cols.append([full[:p], full[p:p + SUB], full[p + SUB:]])
        block = live[p:p + SUB]
        above, below = live[:p], live[p + SUB:]
        for j in range(steps):
            inverse = 1.0 / cols[j][1][j:j + 1, :]
            pivot_row = block[j:j + 1, :] * wide(inverse, tiles)
            for later in range(j + 1, steps):
                c = cols[later]
                scale = c[1][j:j + 1, :] * inverse
                cols[later] = [
                    c[0] - cols[j][0] * scale if p else c[0],
                    jnp.where(rid == j, jnp.broadcast_to(scale, (SUB, LANES)), c[1] - cols[j][1] * scale),
                    c[2] - cols[j][2] * scale if p + SUB < rows else c[2],
                ]
            block = jnp.where(wide(rid, tiles) == j, jnp.broadcast_to(pivot_row, block.shape),
                              block - wide(cols[j][1], tiles) * pivot_row)
            if p:
                above = above - wide(cols[j][0], tiles) * pivot_row
            if p + SUB < rows:
                below = below - wide(cols[j][2], tiles) * pivot_row
        pieces = ([above] if p else []) + [block] + ([below] if p + SUB < rows else [])
        live = jnp.concatenate(pieces, 0) if len(pieces) > 1 else pieces[0]
        system = live if base == 0 else jnp.concatenate([system[:, :base], live], 1)
    return system[:, order:order + 1]


def solve_kernel(total, gram_ref, states_ref, info_ref, grad_ref, inc_ref):
    states = states_ref.shape[2]
    columns = gram_ref.shape[1]
    scale = 1.0 / (total - 1)
    rows, lanes = up(states, SUB), up(states + 1, LANES)
    anom = states_ref[...].astype(F32).reshape(total, states)
    anom = jnp.concatenate([anom, jnp.zeros((total, lanes - states), F32)], 1)
    turned = anom.T[:rows].astype(BF16)
    anom = jnp.concatenate([anom, jnp.zeros((columns - total, lanes), F32)], 0).astype(BF16)
    half = functools.reduce(
        lambda a, b: b + a,
        [jnp.dot(turned, g, preferred_element_type=F32) for g in split3(gram_ref[...])][::-1])
    grad = (half[:, total:total + 1] + half[:, total + 1:total + 2]) * scale
    info = functools.reduce(
        lambda a, b: b + a,
        [jnp.dot(h, anom, preferred_element_type=F32) for h in split3(half)][::-1])
    info = info * (scale * scale)
    info_ref[0] = info[:states, :states]
    rid = lax.broadcasted_iota(jnp.int32, (rows, lanes), 0)
    cid = lax.broadcasted_iota(jnp.int32, (rows, lanes), 1)
    system = info + jnp.where(rid == cid, 1.0, 0.0)
    system = jnp.where(cid == states, jnp.broadcast_to(grad, (rows, lanes)), system)
    step = eliminate(system, states)
    lid = lax.broadcasted_iota(jnp.int32, (rows, LANES), 1)
    pair = jnp.where(lid == 0, grad, jnp.where(lid == 1, step, 0.0))
    pair = jnp.concatenate([pair, jnp.zeros((lanes - rows, LANES), F32)], 0).T
    grad_ref[...] = pair[0:1, :states]
    inc_ref[...] = pair[1:2, :states]


def shards(state_anom, radiance_anom, inv_noise, innovation, valid_count):
    n_mem, n_chan = lax.axis_size("mem"), lax.axis_size("chan")
    members, states = state_anom.shape[1:]
    width = radiance_anom.shape[2]
    total = members * n_mem
    columns = up(total + 16, LANES)
    vmem, anywhere = pl.BlockSpec(memory_space=pltpu.VMEM), pl.BlockSpec(memory_space=pl.ANY)
    dma = pltpu.SemaphoreType.DMA
    gram, own_states = pl.pallas_call(
        functools.partial(gram_kernel, n_mem, n_chan),
        out_shape=(jax.ShapeDtypeStruct((total, columns), F32),
                   jax.ShapeDtypeStruct((n_mem, members, states), BF16)),
        in_specs=[pl.BlockSpec(memory_space=pltpu.SMEM), anywhere, anywhere, vmem, anywhere],
        out_specs=(vmem, vmem),
        scratch_shapes=[
            pltpu.VMEM((n_mem, members, width), BF16),
            pltpu.VMEM((n_mem, members, states), BF16),
            pltpu.VMEM(innovation.shape, F32),
            pltpu.VMEM((n_chan, total, columns), F32),
            dma((3,)), dma((n_mem,)), dma((n_mem,)), dma((n_mem,)), dma((n_mem,)),
            dma((n_chan,)), dma((n_chan,)),
        ],
        compiler_params=pltpu.CompilerParams(
            collective_id=0, has_side_effects=True, vmem_limit_bytes=VMEM_LIMIT),
    )(valid_count, state_anom, radiance_anom, inv_noise[None, :], innovation)
    return pl.pallas_call(
        functools.partial(solve_kernel, total),
        out_shape=(jax.ShapeDtypeStruct((1, states, states), F32),
                   jax.ShapeDtypeStruct((1, states), F32),
                   jax.ShapeDtypeStruct((1, states), F32)),
        in_specs=[vmem, vmem],
        out_specs=(vmem, vmem, vmem),
        compiler_params=pltpu.CompilerParams(vmem_limit_bytes=VMEM_LIMIT),
    )(gram, own_states)


def solution(mesh):
    in_specs = (P(None, "mem", None), P(None, "mem", "chan"), P("chan"), P(None, "chan"), P())
    out_specs = (P("mem", None, None), P("mem", None), P("mem", None))
    return jax.shard_map(shards, mesh=mesh, in_specs=in_specs, out_specs=out_specs, check_vma=False)
```

time: 122 us -> 31 us (0.25)
  other arithmetic: 47.4 us -> 0 us
  waiting for transfers between devices: 28.7 us -> 0 us
  Pallas kernels: 0 us -> 27.1 us
  blocking collectives: 19.9 us -> 0 us
  between operations: 15.5 us -> 0.64 us
  matrix products: 4.67 us -> 0 us
  starting transfers between devices: 3.46 us -> 0 us
    another operation x13 -> x0, other arithmetic: 43.5 us -> none  [the longest x7 23.7 us: shards(): factor = jnp.linalg.cholesky(system)]
    pallas_call x0 -> x2, Pallas kernels: none -> 27.1 us  [the longest x1 19.3 us: shards(): pl.pallas_call(functools.partial(gram_kernel, n_mem, n_chan), out_shape=(...]
    psum x1 -> x0, waiting for transfers between devices: 23.1 us -> none  [shards(): information, gradient = lax.psum((info_share, grad_share), 'chan')]
    all_to_all x1 -> x0, blocking collectives: 14.1 us -> none  [shards(): lax.all_to_all(state_anom, 'mem', split_axis=0, concat_axis=1, tiled=True)]
    psum x1 -> x0, blocking collectives: 5.84 us -> none  [shards(): information, gradient = lax.psum((info_share, grad_share), 'chan')]
    all_to_all x1 -> x0, waiting for transfers between devices: 5.57 us -> none  [shards(): lax.all_to_all(radiance_anom, 'mem', split_axis=0, concat_axis=1, tiled=T...]
    dot_general x3 -> x0, matrix products: 3.46 us -> none  [the longest x1 1.94 us: slab_terms(): jnp.einsum('pcs,pct->pst', weighted, cross, precision=lax.Precision.HIGHEST)]
    all_to_all x1 -> x0, starting transfers between devices: 3.42 us -> none  [shards(): lax.all_to_all(radiance_anom, 'mem', split_axis=0, concat_axis=1, tiled=T...]
  transfers between devices with their start and end apart: 2 -> 0, of which waited for: 2 -> 0; matrix products, arithmetic and copies ran while one was open for 3% -> 0% of each run, Pallas kernels for 0% -> 0%
where the time goes in v1:
time: 31 us; the launch traced here: 30.7 us
  Pallas kernels  27.1 us (87%)
  local copies, waits for them, and re-layouts  3.02 us (10%)
  between operations  0.64 us (2%)
    pallas_call x1, Pallas kernels, shards(): pl.pallas_call(functools.partial(gram_kernel, n_mem, n_chan), out_shape=(...  19.3 us
    pallas_call x1, Pallas kernels, shards(): pl.pallas_call(functools.partial(solve_kernel, total), out_shape=(jax.Sha...  7.73 us
    pallas_call x1, local copies, waits for them, and re-layouts, shards(): pl.pallas_call(functools.partial(solve_kernel, total), out_shape=(jax.Sha...  1.71 us
    broadcast_in_dim x1, local copies, waits for them, and re-layouts, shards(): inv_noise[None, :]  1.31 us

profile of v1, /device:TPU:0, one launch (start us, length us, event | category | flops | bytes accessed | tf_op | source)
XLA Modules:
  0.0 30.7 jit_solution(16275276436296792292)
XLA Ops:
  0.6 1.3 %broadcast_in_dim.3.noise_ref = f32[1,2176]{1,0:T(1,128)} reshape(f32[2176]{0:T(1024)} %param.7) | data formatting | bytes 17408 | tf_op jit(solution)/shard_map/broadcast_in_dim | solution.py:207
  1.9 19.3 %shard_map.76 = (f32[64,128]{1,0:T(8,128)}, bf16[8,8,137]{2,1,0:T(8,128)(2,1)}) custom-call(s32[8]{0:T(128)} %count_ref.1, bf16[8,8,137]{2,1,0:T(8,128)(2,1)} %state_ref.1, bf16[8,8,2176]{2,1,0:T(8,128)(2,1)} %rad_ref.1, f32[1,2176]{1,0:T(1,128)} %broadcast_in_dim.3.noise_ref, f32[8,2176]{1,0:T(8,128)} %innov_ref.1), custom_call_target="tpu_custom_call" | custom-call | tf_op jit(solution)/shard_map/pallas_call | solution.py:191
  21.3 7.7 %shard_map.77 = (f32[1,137,137]{2,1,0:T(8,128)}, f32[1,137]{1,0:T(1,128)}, f32[1,137]{1,0:T(1,128)}) custom-call(f32[64,128]{1,0:T(8,128)} %get-tuple-element.5.gram_ref, bf16[8,8,137]{2,1,0:T(8,128)(2,1)} %get-tuple-element.6.states_ref), custom_call_target="tpu_custom_call" | custom-call | tf_op jit(solution)/shard_map/pallas_call | solution.py:208
  29.0 1.7 %copy.8 = f32[1,137,137]{2,0,1:T(1,128)} copy(f32[1,137,137]{2,1,0:T(8,128)} %get-tuple-element.7) | data formatting | bytes 150152 | tf_op jit(solution)/shard_map/pallas_call | solution.py:208

commit v2 on v1

--- a/solution.py
+++ b/solution.py
@@ -8,6 +8,7 @@
 
 F32, BF16 = jnp.float32, jnp.bfloat16
 LANES, SUB = 128, 8
+PARTS = 4
 VMEM_LIMIT = 60 * 1024 * 1024
 
 
@@ -23,7 +24,13 @@
     return a, b, c
 
 
-def gram_kernel(n_mem, n_chan, count_ref, state_ref, rad_ref, noise_ref, innov_ref,
+def pieces(width, count):
+    tiles = width // LANES
+    marks = [(tiles - tiles * i // count) * LANES for i in range(count, 0, -1)] + [width]
+    return list(zip(marks[:-1], marks[1:]))
+
+
+def gram_kernel(n_mem, n_chan, parts_of_slab, count_ref, state_ref, rad_ref, noise_ref, innov_ref,
                 gram_ref, states_ref, held, held_states, innov, parts,
                 local_sem, send_sem, recv_sem, ssend_sem, srecv_sem, psend_sem, precv_sem):
     me, slab = lax.axis_index("mem"), lax.axis_index("chan")
@@ -46,50 +53,54 @@
         copy.start()
     pl.semaphore_wait(barrier, n_mem - 1 + n_chan - 1)
 
-    sends = []
+    cuts = pieces(width, parts_of_slab)
+    sends, late = [], []
+    for c, (lo, hi) in enumerate(cuts):
+        for k in range(n_mem - 1, 0, -1):
+            peer = lax.rem(me + k, n_mem)
+            late.append(pltpu.make_async_remote_copy(
+                src_ref=rad_ref.at[peer, :, lo:hi], dst_ref=held.at[k, :, lo:hi],
+                send_sem=send_sem.at[c, k], recv_sem=recv_sem.at[c, k], device_id={"mem": peer}))
+            late[-1].start()
+        sends.append(late)
+        late = []
+    small = []
     for k in range(1, n_mem):
         peer = lax.rem(me + k, n_mem)
-        sends.append(pltpu.make_async_remote_copy(
-            src_ref=rad_ref.at[peer], dst_ref=held.at[k],
-            send_sem=send_sem.at[k], recv_sem=recv_sem.at[k], device_id={"mem": peer}))
-        sends[-1].start()
-    for k in range(1, n_mem):
-        peer = lax.rem(me + k, n_mem)
-        sends.append(pltpu.make_async_remote_copy(
+        small.append(pltpu.make_async_remote_copy(
             src_ref=state_ref.at[peer], dst_ref=held_states.at[k],
             send_sem=ssend_sem.at[k], recv_sem=srecv_sem.at[k], device_id={"mem": peer}))
-        sends[-1].start()
+        small[-1].start()
 
     for copy in own:
         copy.wait()
     slots = slab * width + lax.broadcasted_iota(jnp.int32, (1, width), 1)
-    weight = jnp.where(slots < count_ref[me], noise_ref[...], 0.0)
+    weight = jnp.where(slots < count_ref[me], noise_ref[...].reshape(1, width), 0.0)
     pull = weight * innov[pl.ds(me, 1), :]
     pull = [part.astype(F32) for part in split3(pull)]
-    for copy in sends:
-        copy.wait_recv()
-
     extra = columns - total
     row = lax.broadcasted_iota(jnp.int32, (extra, 1), 0)
     acc = jnp.zeros((total, columns), F32)
     step = 2 * LANES
-    for lo in range(0, width, step):
-        hi = min(lo + step, width)
-        block = held[:, :, lo:hi].astype(F32).reshape(total, hi - lo)
-        scaled = block * weight[:, lo:hi]
-        first = scaled.astype(BF16)
-        second = (scaled - first.astype(F32)).astype(BF16)
-        p0, p1, p2 = (part[:, lo:hi] for part in pull)
-        tail0 = jnp.where(row == 0, p0, jnp.where(row == 1, p2, 0.0)).astype(BF16)
-        tail1 = jnp.where(row == 0, p1, 0.0).astype(BF16)
-        block = block.astype(BF16)
-        dims = (((1,), (1,)), ((), ()))
-        acc += (
-            lax.dot_general(block, jnp.concatenate([first, tail0], 0), dims, preferred_element_type=F32)
-            + lax.dot_general(block, jnp.concatenate([second, tail1], 0), dims, preferred_element_type=F32)
-        )
+    for (start, stop), copies in zip(cuts, sends):
+        for copy in copies:
+            copy.wait_recv()
+        for lo in range(start, stop, step):
+            hi = min(lo + step, stop)
+            block = held[:, :, lo:hi].astype(F32).reshape(total, hi - lo)
+            scaled = block * weight[:, lo:hi]
+            first = scaled.astype(BF16)
+            second = (scaled - first.astype(F32)).astype(BF16)
+            p0, p1, p2 = (part[:, lo:hi] for part in pull)
+            tail0 = jnp.where(row == 0, p0, jnp.where(row == 1, p2, 0.0)).astype(BF16)
+            tail1 = jnp.where(row == 0, p1, 0.0).astype(BF16)
+            block = block.astype(BF16)
+            dims = (((1,), (1,)), ((), ()))
+            acc += (
+                lax.dot_general(block, jnp.concatenate([first, tail0], 0), dims, preferred_element_type=F32)
+                + lax.dot_general(block, jnp.concatenate([second, tail1], 0), dims, preferred_element_type=F32)
+            )
     parts[slab] = acc
-    states_ref[...] = held_states[...]
 
     shares = []
     for k in range(1, n_chan):
@@ -98,7 +109,10 @@
             src_ref=parts.at[slab], dst_ref=parts.at[slab],
             send_sem=psend_sem.at[k], recv_sem=precv_sem.at[k], device_id={"chan": peer}))
         shares[-1].start()
-    for copy in sends:
+    for copy in small:
+        copy.wait_recv()
+    states_ref[...] = held_states[...]
+    for copy in small + sum(sends, []):
         copy.wait_send()
     for copy in shares:
         copy.wait()
@@ -167,7 +181,7 @@
         lambda a, b: b + a,
         [jnp.dot(h, anom, preferred_element_type=F32) for h in split3(half)][::-1])
     info = info * (scale * scale)
-    info_ref[0] = info[:states, :states]
+    info_ref[:, 0, :] = info[:states, :states]
     rid = lax.broadcasted_iota(jnp.int32, (rows, lanes), 0)
     cid = lax.broadcasted_iota(jnp.int32, (rows, lanes), 1)
     system = info + jnp.where(rid == cid, 1.0, 0.0)
@@ -189,7 +203,7 @@
     vmem, anywhere = pl.BlockSpec(memory_space=pltpu.VMEM), pl.BlockSpec(memory_space=pl.ANY)
     dma = pltpu.SemaphoreType.DMA
     gram, own_states = pl.pallas_call(
-        functools.partial(gram_kernel, n_mem, n_chan),
+        functools.partial(gram_kernel, n_mem, n_chan, PARTS),
         out_shape=(jax.ShapeDtypeStruct((total, columns), F32),
                    jax.ShapeDtypeStruct((n_mem, members, states), BF16)),
         in_specs=[pl.BlockSpec(memory_space=pltpu.SMEM), anywhere, anywhere, vmem, anywhere],
@@ -199,21 +213,22 @@
             pltpu.VMEM((n_mem, members, states), BF16),
             pltpu.VMEM(innovation.shape, F32),
             pltpu.VMEM((n_chan, total, columns), F32),
-            dma((3,)), dma((n_mem,)), dma((n_mem,)), dma((n_mem,)), dma((n_mem,)),
+            dma((3,)), dma((PARTS, n_mem)), dma((PARTS, n_mem)), dma((n_mem,)), dma((n_mem,)),
             dma((n_chan,)), dma((n_chan,)),
         ],
         compiler_params=pltpu.CompilerParams(
             collective_id=0, has_side_effects=True, vmem_limit_bytes=VMEM_LIMIT),
-    )(valid_count, state_anom, radiance_anom, inv_noise[None, :], innovation)
-    return pl.pallas_call(
+    )(valid_count, state_anom, radiance_anom, inv_noise, innovation)
+    information, gradient, increment = pl.pallas_call(
         functools.partial(solve_kernel, total),
-        out_shape=(jax.ShapeDtypeStruct((1, states, states), F32),
+        out_shape=(jax.ShapeDtypeStruct((states, 1, states), F32),
                    jax.ShapeDtypeStruct((1, states), F32),
                    jax.ShapeDtypeStruct((1, states), F32)),
         in_specs=[vmem, vmem],
         out_specs=(vmem, vmem, vmem),
         compiler_params=pltpu.CompilerParams(vmem_limit_bytes=VMEM_LIMIT),
     )(gram, own_states)
+    return information.transpose(1, 0, 2), gradient, increment
 
 
 def solution(mesh):

time: 31 us -> 28.2 us (0.910)
  local copies, waits for them, and re-layouts: 3.02 us -> 0 us
    pallas_call x1 -> x0, local copies, waits for them, and re-layouts: 1.71 us -> none  [shards(): pl.pallas_call(functools.partial(solve_kernel, total), out_shape=(jax.Sha...]
    broadcast_in_dim x1 -> x0, local copies, waits for them, and re-layouts: 1.31 us -> none  [shards(): inv_noise[None, :]]
where the time goes in v2:
time: 28.2 us; the launch traced here: 27.9 us
  Pallas kernels  27.3 us (97%)
  between operations  0.64 us (2%)
    pallas_call x1, Pallas kernels, shards(): pl.pallas_call(functools.partial(gram_kernel, n_mem, n_chan, PARTS), out_...  19.5 us
    pallas_call x1, Pallas kernels, shards(): pl.pallas_call(functools.partial(solve_kernel, total), out_shape=(jax.Sha...  7.74 us

profile of v2, /device:TPU:0, one launch (start us, length us, event | category | flops | bytes accessed | tf_op | source)
XLA Modules:
  0.0 27.9 jit_solution(2754173420064629606)
XLA Ops:
  0.6 19.5 %shard_map.76 = (f32[64,128]{1,0:T(8,128)}, bf16[8,8,137]{2,1,0:T(8,128)(2,1)}) custom-call(s32[8]{0:T(128)} %count_ref.1, bf16[8,8,137]{2,1,0:T(8,128)(2,1)} %state_ref.1, bf16[8,8,2176]{2,1,0:T(8,128)(2,1)} %rad_ref.1, f32[2176]{0:T(1024)} %noise_ref.1, f32[8,2176]{1,0:T(8,128)} %innov_ref.1), custom_call_target="tpu_custom_call" | custom-call | tf_op jit(solution)/shard_map/pallas_call | solution.py:205
  20.2 7.7 %shard_map.77 = (f32[137,1,137]{2,1,0:T(1,128)}, f32[1,137]{1,0:T(1,128)}, f32[1,137]{1,0:T(1,128)}) custom-call(f32[64,128]{1,0:T(8,128)} %get-tuple-element.8.gram_ref, bf16[8,8,137]{2,1,0:T(8,128)(2,1)} %get-tuple-element.9.states_ref), custom_call_target="tpu_custom_call" | custom-call | tf_op jit(solution)/shard_map/pallas_call | solution.py:222

commit v3 on v2

--- a/solution.py
+++ b/solution.py
@@ -9,6 +9,7 @@
 F32, BF16 = jnp.float32, jnp.bfloat16
 LANES, SUB = 128, 8
 PARTS = 4
+TINY = 2e-38
 VMEM_LIMIT = 60 * 1024 * 1024
 
 
@@ -30,9 +31,37 @@
     return list(zip(marks[:-1], marks[1:]))
 
 
+def orthogonalise(anom, vectors_ref, lower_ref):
+    total, states = anom.shape
+    lanes = vectors_ref.shape[1]
+    anom = jnp.concatenate([anom, jnp.zeros((total, lanes - states), F32)], 1)
+    cid = lax.broadcasted_iota(jnp.int32, lower_ref.shape, 1)
+    rid = lax.broadcasted_iota(jnp.int32, lower_ref.shape, 0)
+    lower = jnp.zeros(lower_ref.shape, F32)
+    for k in range(total):
+        top = k // SUB * SUB
+        live = anom[top:]
+        vector = anom[k:k + 1]
+        dots = jnp.sum(live * vector, axis=1, keepdims=True)
+        norm = dots[k - top:k - top + 1]
+        inverse = jnp.where(norm > TINY, 1.0 / norm, 0.0)
+        after = lax.broadcasted_iota(jnp.int32, (total - top, 1), 0) > k - top
+        live = live - jnp.where(after, dots * inverse, 0.0) * vector
+        pad = [] if top == 0 else [jnp.zeros((top, 1), F32)]
+        lower = jnp.where((cid == k) & (rid >= k), jnp.concatenate(pad + [dots], 0), lower)
+        anom = live if top == 0 else jnp.concatenate([anom[:top], live], 0)
+    diagonal = jnp.where(cid == rid, lower, 0.0)
+    across = jnp.sum(diagonal, axis=0, keepdims=True)
+    down = jnp.sum(diagonal, axis=1, keepdims=True)
+    lower_ref[...] = lower * jnp.where(across > TINY, lax.rsqrt(across), 0.0)
+    vectors_ref[...] = anom * jnp.where(down > TINY, lax.rsqrt(down), 0.0)
+
+
 def gram_kernel(n_mem, n_chan, parts_of_slab, count_ref, state_ref, rad_ref, noise_ref, innov_ref,
-                gram_ref, states_ref, held, held_states, innov, parts,
-                local_sem, send_sem, recv_sem, ssend_sem, srecv_sem, psend_sem, precv_sem):
+                gram_ref, states_ref, *rest):
+    basis_refs = rest[:-11]
+    (held, held_states, innov, parts,
+     local_sem, send_sem, recv_sem, ssend_sem, srecv_sem, psend_sem, precv_sem) = rest[-11:]
     me, slab = lax.axis_index("mem"), lax.axis_index("chan")
     members = rad_ref.shape[1]
     width = rad_ref.shape[2]
@@ -51,8 +80,21 @@
     ]
     for copy in own:
         copy.start()
+    for copy in own:
+        copy.wait()
+    slots = slab * width + lax.broadcasted_iota(jnp.int32, (1, width), 1)
+    weight = jnp.where(slots < count_ref[me], noise_ref[...].reshape(1, width), 0.0)
+    pull = weight * innov[pl.ds(me, 1), :]
+    pull = [part.astype(F32) for part in split3(pull)]
     pl.semaphore_wait(barrier, n_mem - 1 + n_chan - 1)
 
+    small = []
+    for k in range(1, n_mem):
+        peer = lax.rem(me + k, n_mem)
+        small.append(pltpu.make_async_remote_copy(
+            src_ref=state_ref.at[peer], dst_ref=held_states.at[k],
+            send_sem=ssend_sem.at[k], recv_sem=srecv_sem.at[k], device_id={"mem": peer}))
+        small[-1].start()
     cuts = pieces(width, parts_of_slab)
     sends, late = [], []
     for c, (lo, hi) in enumerate(cuts):
@@ -64,20 +106,11 @@
             late[-1].start()
         sends.append(late)
         late = []
-    small = []
-    for k in range(1, n_mem):
-        peer = lax.rem(me + k, n_mem)
-        small.append(pltpu.make_async_remote_copy(
-            src_ref=state_ref.at[peer], dst_ref=held_states.at[k],
-            send_sem=ssend_sem.at[k], recv_sem=srecv_sem.at[k], device_id={"mem": peer}))
-        small[-1].start()
-
-    for copy in own:
-        copy.wait()
-    slots = slab * width + lax.broadcasted_iota(jnp.int32, (1, width), 1)
-    weight = jnp.where(slots < count_ref[me], noise_ref[...].reshape(1, width), 0.0)
-    pull = weight * innov[pl.ds(me, 1), :]
-    pull = [part.astype(F32) for part in split3(pull)]
+    for copy in small:
+        copy.wait_recv()
+    states_ref[...] = held_states[...]
+    if basis_refs:
+        orthogonalise(held_states[...].astype(F32).reshape(total, held_states.shape[2]), *basis_refs)
     extra = columns - total
     row = lax.broadcasted_iota(jnp.int32, (extra, 1), 0)
     acc = jnp.zeros((total, columns), F32)
@@ -109,9 +142,6 @@
             src_ref=parts.at[slab], dst_ref=parts.at[slab],
             send_sem=psend_sem.at[k], recv_sem=precv_sem.at[k], device_id={"chan": peer}))
         shares[-1].start()
-    for copy in small:
-        copy.wait_recv()
-    states_ref[...] = held_states[...]
     for copy in small + sum(sends, []):
         copy.wait_send()
     for copy in shares:
@@ -164,33 +194,52 @@
     return system[:, order:order + 1]
 
 
-def solve_kernel(total, gram_ref, states_ref, info_ref, grad_ref, inc_ref):
+def solve_kernel(total, gram_ref, states_ref, *rest):
+    basis_refs, (info_ref, grad_ref, inc_ref) = rest[:-3], rest[-3:]
     states = states_ref.shape[2]
     columns = gram_ref.shape[1]
     scale = 1.0 / (total - 1)
     rows, lanes = up(states, SUB), up(states + 1, LANES)
     anom = states_ref[...].astype(F32).reshape(total, states)
     anom = jnp.concatenate([anom, jnp.zeros((total, lanes - states), F32)], 1)
+    gram = gram_ref[...]
+    force = (gram[:, total:total + 1] + gram[:, total + 1:total + 2]) * scale
+    grad_ref[...] = jnp.sum(force * anom, axis=0, keepdims=True)[:, :states]
+    if basis_refs:
+        vectors_ref, lower_ref = basis_refs
+        lower = lower_ref[...]
+        order = lower.T[:total]
+        mixed = jnp.dot(order, gram, precision=lax.Precision.HIGHEST, preferred_element_type=F32)
+        right = (mixed[:, total:total + 1] + mixed[:, total + 1:total + 2]) * scale
+        full = jnp.concatenate([lower, jnp.zeros((columns - total, lower.shape[1]), F32)], 0)
+        system = jnp.dot(mixed, full, precision=lax.Precision.HIGHEST, preferred_element_type=F32) * (scale * scale)
+        rid = lax.broadcasted_iota(jnp.int32, system.shape, 0)
+        cid = lax.broadcasted_iota(jnp.int32, system.shape, 1)
+        system = system + jnp.where(rid == cid, 1.0, 0.0)
+        system = jnp.where(cid == total, jnp.broadcast_to(right, system.shape), system)
+        step = eliminate(system, total)
+        inc_ref[...] = jnp.sum(step * vectors_ref[...], axis=0, keepdims=True)[:, :states]
     turned = anom.T[:rows].astype(BF16)
     anom = jnp.concatenate([anom, jnp.zeros((columns - total, lanes), F32)], 0).astype(BF16)
     half = functools.reduce(
         lambda a, b: b + a,
-        [jnp.dot(turned, g, preferred_element_type=F32) for g in split3(gram_ref[...])][::-1])
+        [jnp.dot(turned, g, preferred_element_type=F32) for g in split3(gram)][::-1])
     grad = (half[:, total:total + 1] + half[:, total + 1:total + 2]) * scale
     info = functools.reduce(
         lambda a, b: b + a,
         [jnp.dot(h, anom, preferred_element_type=F32) for h in split3(half)][::-1])
     info = info * (scale * scale)
     info_ref[:, 0, :] = info[:states, :states]
+    if basis_refs:
+        return
     rid = lax.broadcasted_iota(jnp.int32, (rows, lanes), 0)
     cid = lax.broadcasted_iota(jnp.int32, (rows, lanes), 1)
     system = info + jnp.where(rid == cid, 1.0, 0.0)
     system = jnp.where(cid == states, jnp.broadcast_to(grad, (rows, lanes)), system)
     step = eliminate(system, states)
     lid = lax.broadcasted_iota(jnp.int32, (rows, LANES), 1)
-    pair = jnp.where(lid == 0, grad, jnp.where(lid == 1, step, 0.0))
+    pair = jnp.where(lid == 1, step, 0.0)
     pair = jnp.concatenate([pair, jnp.zeros((lanes - rows, LANES), F32)], 0).T
-    grad_ref[...] = pair[0:1, :states]
     inc_ref[...] = pair[1:2, :states]
 
 
@@ -202,12 +251,14 @@
     columns = up(total + 16, LANES)
     vmem, anywhere = pl.BlockSpec(memory_space=pltpu.VMEM), pl.BlockSpec(memory_space=pl.ANY)
     dma = pltpu.SemaphoreType.DMA
-    gram, own_states = pl.pallas_call(
+    basis = () if total > states else (jax.ShapeDtypeStruct((total, up(states + 1, LANES)), F32),
+                                       jax.ShapeDtypeStruct((total, up(total + 1, LANES)), F32))
+    gram, own_states, *bases = pl.pallas_call(
         functools.partial(gram_kernel, n_mem, n_chan, PARTS),
         out_shape=(jax.ShapeDtypeStruct((total, columns), F32),
-                   jax.ShapeDtypeStruct((n_mem, members, states), BF16)),
+                   jax.ShapeDtypeStruct((n_mem, members, states), BF16)) + basis,
         in_specs=[pl.BlockSpec(memory_space=pltpu.SMEM), anywhere, anywhere, vmem, anywhere],
-        out_specs=(vmem, vmem),
+        out_specs=(vmem,) * (2 + len(basis)),
         scratch_shapes=[
             pltpu.VMEM((n_mem, members, width), BF16),
             pltpu.VMEM((n_mem, members, states), BF16),
@@ -224,10 +275,10 @@
         out_shape=(jax.ShapeDtypeStruct((states, 1, states), F32),
                    jax.ShapeDtypeStruct((1, states), F32),
                    jax.ShapeDtypeStruct((1, states), F32)),
-        in_specs=[vmem, vmem],
+        in_specs=[vmem] * (2 + len(basis)),
         out_specs=(vmem, vmem, vmem),
         compiler_params=pltpu.CompilerParams(vmem_limit_bytes=VMEM_LIMIT),
-    )(gram, own_states)
+    )(gram, own_states, *bases)
     return information.transpose(1, 0, 2), gradient, increment
 
 

time: 28.2 us -> 26.2 us (0.929)
  Pallas kernels: 27.3 us -> 25.3 us
    pallas_call x1, Pallas kernels: 7.74 us -> 3.51 us  [shards(): pl.pallas_call(functools.partial(solve_kernel, total), out_shape=(jax.Sha...]
    pallas_call x1, Pallas kernels: 19.5 us -> 21.8 us  [shards(): pl.pallas_call(functools.partial(gram_kernel, n_mem, n_chan, PARTS), out_...]
where the time goes in v3:
time: 26.2 us; the launch traced here: 25.9 us
  Pallas kernels  25.3 us (97%)
  between operations  0.64 us (2%)
    pallas_call x1, Pallas kernels, shards(): pl.pallas_call(functools.partial(gram_kernel, n_mem, n_chan, PARTS), out_...  21.8 us
    pallas_call x1, Pallas kernels, shards(): pl.pallas_call(functools.partial(solve_kernel, total), out_shape=(jax.Sha...  3.51 us

profile of v3, /device:TPU:0, one launch (start us, length us, event | category | flops | bytes accessed | tf_op | source)
XLA Modules:
  0.0 25.9 jit_solution(2847903758203201730)
XLA Ops:
  0.6 21.8 %shard_map.76 = (f32[64,128]{1,0:T(8,128)}, bf16[8,8,137]{2,1,0:T(8,128)(2,1)}, f32[64,256]{1,0:T(8,128)}, f32[64,128]{1,0:T(8,128)}) custom-call(s32[8]{0:T(128)} %count_ref.1, bf16[8,8,137]{2,1,0:T(8,128)(2,1)} %state_ref.1, bf16[8,8,2176]{2,1,0:T(8,128)(2,1)} %rad_ref.1, f32[2176]{0:T(1024)} %noise_ref.1, f32[8,2176]{1,0:T(8,128)} %innov_ref.1), custom_call_target="tpu_custom_call" | custom-call | tf_op jit(solution)/shard_map/pallas_call | solution.py:256
  22.4 3.5 %shard_map.77 = (f32[137,1,137]{2,1,0:T(1,128)}, f32[1,137]{1,0:T(1,128)}, f32[1,137]{1,0:T(1,128)}) custom-call(f32[64,128]{1,0:T(8,128)} %get-tuple-element.10.gram_ref, bf16[8,8,137]{2,1,0:T(8,128)(2,1)} %get-tuple-element.11.states_ref, f32[64,256]{1,0:T(8,128)} %get-tuple-element.12.rest_0_, f32[64,128]{1,0:T(8,128)} %get-tuple-element.13.rest_1_), custom_call_target="tpu_custom_call" | custom-call | tf_op jit(solution)/shard_map/pallas_call | solution.py:273

commit v4 on v3

--- a/solution.py
+++ b/solution.py
@@ -31,14 +31,12 @@
     return list(zip(marks[:-1], marks[1:]))
 
 
-def orthogonalise(anom, vectors_ref, lower_ref):
-    total, states = anom.shape
-    lanes = vectors_ref.shape[1]
-    anom = jnp.concatenate([anom, jnp.zeros((total, lanes - states), F32)], 1)
-    cid = lax.broadcasted_iota(jnp.int32, lower_ref.shape, 1)
-    rid = lax.broadcasted_iota(jnp.int32, lower_ref.shape, 0)
-    lower = jnp.zeros(lower_ref.shape, F32)
-    for k in range(total):
+def orthogonalise(state, first, last):
+    anom, lower = state
+    total = anom.shape[0]
+    cid = lax.broadcasted_iota(jnp.int32, lower.shape, 1)
+    rid = lax.broadcasted_iota(jnp.int32, lower.shape, 0)
+    for k in range(first, last):
         top = k // SUB * SUB
         live = anom[top:]
         vector = anom[k:k + 1]
@@ -50,6 +48,13 @@
         pad = [] if top == 0 else [jnp.zeros((top, 1), F32)]
         lower = jnp.where((cid == k) & (rid >= k), jnp.concatenate(pad + [dots], 0), lower)
         anom = live if top == 0 else jnp.concatenate([anom[:top], live], 0)
+    return anom, lower
+
+
+def normalise(state, vectors_ref, lower_ref):
+    anom, lower = state
+    cid = lax.broadcasted_iota(jnp.int32, lower.shape, 1)
+    rid = lax.broadcasted_iota(jnp.int32, lower.shape, 0)
     diagonal = jnp.where(cid == rid, lower, 0.0)
     across = jnp.sum(diagonal, axis=0, keepdims=True)
     down = jnp.sum(diagonal, axis=1, keepdims=True)
@@ -110,7 +115,11 @@
         copy.wait_recv()
     states_ref[...] = held_states[...]
     if basis_refs:
-        orthogonalise(held_states[...].astype(F32).reshape(total, held_states.shape[2]), *basis_refs)
+        anom = held_states[...].astype(F32).reshape(total, held_states.shape[2])
+        spare = jnp.zeros((total, basis_refs[0].shape[1] - anom.shape[1]), F32)
+        basis = jnp.concatenate([anom, spare], 1), jnp.zeros(basis_refs[1].shape, F32)
+        early = total * 7 // 16
+        basis = orthogonalise(basis, 0, early)
     extra = columns - total
     row = lax.broadcasted_iota(jnp.int32, (extra, 1), 0)
     acc = jnp.zeros((total, columns), F32)
@@ -142,6 +151,8 @@
             src_ref=parts.at[slab], dst_ref=parts.at[slab],
             send_sem=psend_sem.at[k], recv_sem=precv_sem.at[k], device_id={"chan": peer}))
         shares[-1].start()
+    if basis_refs:
+        normalise(orthogonalise(basis, early, total), *basis_refs)
     for copy in small + sum(sends, []):
         copy.wait_send()
     for copy in shares:

time: 26.2 us -> 27.2 us (1.038)
  Pallas kernels: 25.3 us -> 26.3 us
    pallas_call x1, Pallas kernels: 21.8 us -> 22.8 us  [shards(): pl.pallas_call(functools.partial(gram_kernel, n_mem, n_chan, PARTS), out_...]
where the time goes in v4:
time: 27.2 us; the launch traced here: 27 us
  Pallas kernels  26.3 us (97%)
  between operations  0.64 us (2%)
    pallas_call x1, Pallas kernels, shards(): pl.pallas_call(functools.partial(gram_kernel, n_mem, n_chan, PARTS), out_...  22.8 us
    pallas_call x1, Pallas kernels, shards(): pl.pallas_call(functools.partial(solve_kernel, total), out_shape=(jax.Sha...  3.51 us

profile of v4, /device:TPU:0, one launch (start us, length us, event | category | flops | bytes accessed | tf_op | source)
XLA Modules:
  0.0 27.0 jit_solution(9494984694806716228)
XLA Ops:
  0.6 22.8 %shard_map.76 = (f32[64,128]{1,0:T(8,128)}, bf16[8,8,137]{2,1,0:T(8,128)(2,1)}, f32[64,256]{1,0:T(8,128)}, f32[64,128]{1,0:T(8,128)}) custom-call(s32[8]{0:T(128)} %count_ref.1, bf16[8,8,137]{2,1,0:T(8,128)(2,1)} %state_ref.1, bf16[8,8,2176]{2,1,0:T(8,128)(2,1)} %rad_ref.1, f32[2176]{0:T(1024)} %noise_ref.1, f32[8,2176]{1,0:T(8,128)} %innov_ref.1), custom_call_target="tpu_custom_call" | custom-call | tf_op jit(solution)/shard_map/pallas_call | solution.py:267
  23.5 3.5 %shard_map.77 = (f32[137,1,137]{2,1,0:T(1,128)}, f32[1,137]{1,0:T(1,128)}, f32[1,137]{1,0:T(1,128)}) custom-call(f32[64,128]{1,0:T(8,128)} %get-tuple-element.10.gram_ref, bf16[8,8,137]{2,1,0:T(8,128)(2,1)} %get-tuple-element.11.states_ref, f32[64,256]{1,0:T(8,128)} %get-tuple-element.12.rest_0_, f32[64,128]{1,0:T(8,128)} %get-tuple-element.13.rest_1_), custom_call_target="tpu_custom_call" | custom-call | tf_op jit(solution)/shard_map/pallas_call | solution.py:284
